TPU v7x, 32 devices: a whole 2x2x4 slice. The times are simulated.
32 devices in a mesh: dp: 4 (over y, x), context: 4 (over z), head: 2 (over core).
Axes of the slice: x: 2, y: 2, z: 4, core: 2. Of those that a mesh axis runs over, the one named last changes fastest.
Arguments:
- tokens: bfloat16 [4, 2, 512, 4096], P('dp', None, 'context', 'head'), may hold values from -7 to 7
- queries: bfloat16 [4, 2, 512, 2048], P('dp', None, 'context', 'head'), may hold values from -160 to 160
- grad_out: bfloat16 [4, 2, 512, 2048], P('dp', None, 'context', 'head'), may hold values from -6 to 6
- w_key: bfloat16 [4096, 256], P('context', 'head'), may hold values from -0.09375 to 0.09375
- w_value: bfloat16 [4096, 256], P('context', 'head'), may hold values from -0.09375 to 0.09375
- block_len: int32 [4], P('dp'), may hold values from 8 to 32, as said below
Outputs:
- grad_query: bfloat16 [4, 2, 512, 2048], P('dp', None, 'context', 'head')
- grad_x: bfloat16 [4, 2, 512, 4096], P('dp', None, 'context', 'head')
- grad_wkey: float32 [4096, 256], P('context', 'head')
- grad_wvalue: float32 [4096, 256], P('context', 'head')
Inputs may be any that keep to these rules, and one draw needn't show every extreme that they name: `block_len`: each entry is 8, 16 or 32.
All inputs are finite; a program needn't handle non-finite values.
Results may differ from a plain program's by a relative error of at most 0.025.
Values may be sent and summed in bfloat16 or wider, within the bound.
A program may use at most 64 MiB of HBM per device.

v0:
```python
import math
import jax
import jax.numpy as jnp
from jax import lax
from jax.sharding import PartitionSpec as P

HEAD_DIM = 128
masked_score = -1e30


def score_block(query_rows, key_rows, score_scale):
    return (
        jnp.einsum("ikgd,jkd->kgij", query_rows, key_rows, preferred_element_type=jnp.float32)
        * score_scale
    )


def visible_mask(query_pos, key_pos, block_size, strict):
    query_block = query_pos // block_size
    key_block = key_pos // block_size
    if strict:
        return key_block[None, :] < query_block[:, None]
    return key_block[None, :] <= query_block[:, None]


def forward_step(carried, query_rows, key_rows, value_rows, allowed_mask, score_scale):
    row_peak, row_total, weighted = carried
    logits = jnp.where(allowed_mask, score_block(query_rows, key_rows, score_scale), masked_score)
    new_peak = jnp.maximum(row_peak, jnp.max(logits, axis=-1))
    shrink = jnp.exp(row_peak - new_peak)
    weights = jnp.where(allowed_mask, jnp.exp(logits - new_peak[..., None]), 0.0)
    row_total = row_total * shrink + jnp.sum(weights, axis=-1)
    update = jnp.einsum(
        "kgij,jkd->kgid",
        weights.astype(jnp.bfloat16),
        value_rows,
        preferred_element_type=jnp.float32,
    )
    return (new_peak, row_total, weighted * shrink[..., None] + update)


def backward_step(
    query_rows, grad_rows, key_rows, value_rows, allowed_mask, log_total, row_delta, score_scale
):
    logits = jnp.where(allowed_mask, score_block(query_rows, key_rows, score_scale), masked_score)
    probs = jnp.exp(logits - log_total[..., None])
    probs_half = probs.astype(jnp.bfloat16)
    grad_probs = jnp.einsum(
        "ikgd,jkd->kgij", grad_rows, value_rows, preferred_element_type=jnp.float32
    )
    grad_logits = (probs * (grad_probs - row_delta[..., None])).astype(jnp.bfloat16)
    grad_rows_query = jnp.einsum(
        "kgij,jkd->ikgd", grad_logits, key_rows, preferred_element_type=jnp.float32
    )
    grad_key = (
        jnp.einsum("kgij,ikgd->jkd", grad_logits, query_rows, preferred_element_type=jnp.float32)
        * score_scale
    )
    grad_value = jnp.einsum(
        "kgij,ikgd->jkd", probs_half, grad_rows, preferred_element_type=jnp.float32
    )
    return (grad_rows_query, grad_key, grad_value)


def finish_rows(carried, grad_rows):
    row_peak, row_total, weighted = carried
    outputs = weighted / row_total[..., None]
    row_delta = jnp.einsum("ikgd,kgid->kgi", grad_rows.astype(jnp.float32), outputs)
    return (row_peak + jnp.log(row_total), row_delta)


def per_device(tokens, queries, grad_out, w_key, w_value, block_len):
    cycle_size = lax.axis_size("context")
    my_index = lax.axis_index("context")
    shard_rows = tokens.shape[2]
    kv_width = w_key.shape[1]
    kv_local = kv_width // HEAD_DIM
    query_width = queries.shape[3]
    group_size = query_width // HEAD_DIM // kv_local
    score_scale = 1.0 / math.sqrt(HEAD_DIM)
    block_size = block_len[0]
    local_pos = lax.iota(jnp.int32, shard_rows)
    span_rows = min(cycle_size * shard_rows, max(512, shard_rows))
    full_tokens = lax.all_gather(
        tokens[0].reshape(2 * shard_rows, tokens.shape[3]), "head", axis=1, tiled=True
    )
    weight_pair = jnp.concatenate([w_key, w_value], axis=1)
    columns = full_tokens
    projected = jnp.dot(
        columns,
        lax.all_gather(weight_pair, "context", axis=0, tiled=True),
        preferred_element_type=jnp.float32,
    ).astype(jnp.bfloat16)
    clean_pairs = projected[:shard_rows]
    q_clean = queries[0, 0].reshape(shard_rows, kv_local, group_size, HEAD_DIM)
    g_clean = grad_out[0, 0].reshape(shard_rows, kv_local, group_size, HEAD_DIM)
    noisy_bundle = jnp.concatenate([queries[0, 1], grad_out[0, 1], projected[shard_rows:]], axis=1)
    q_noisy = noisy_bundle[:, :query_width].reshape(shard_rows, kv_local, group_size, HEAD_DIM)
    g_noisy = noisy_bundle[:, query_width : 2 * query_width].reshape(
        shard_rows, kv_local, group_size, HEAD_DIM
    )
    k_noisy = noisy_bundle[:, 2 * query_width : 2 * query_width + kv_width].reshape(
        shard_rows, kv_local, HEAD_DIM
    )
    v_noisy = noisy_bundle[:, 2 * query_width + kv_width :].reshape(shard_rows, kv_local, HEAD_DIM)
    clean_pos = my_index * shard_rows + local_pos
    noisy_pos = my_index * shard_rows + local_pos
    own_block = local_pos // block_size
    same_block = own_block[None, :] == own_block[:, None]
    clean_limit = (my_index + 1) * shard_rows
    noisy_limit = (my_index + 1) * shard_rows
    state_shape = (kv_local, group_size, shard_rows)
    empty_state = (
        jnp.full(state_shape, masked_score, jnp.float32),
        jnp.zeros(state_shape, jnp.float32),
        jnp.zeros(state_shape + (HEAD_DIM,), jnp.float32),
    )
    noisy_start = forward_step(empty_state, q_noisy, k_noisy, v_noisy, same_block, score_scale)
    block_turns = (jnp.maximum(clean_limit, noisy_limit) + span_rows - 1) // span_rows

    def split_pairs(pair_rows):
        count_rows = pair_rows.shape[0]
        key_rows = pair_rows[:, :kv_width].reshape(count_rows, kv_local, HEAD_DIM)
        value_rows = pair_rows[:, kv_width:].reshape(count_rows, kv_local, HEAD_DIM)
        return (key_rows, value_rows)

    carried = (empty_state, noisy_start)
    pair_rows = lax.all_gather(clean_pairs, "context", axis=0, tiled=True)
    first_row = jnp.int32(0)
    key_rows, value_rows = split_pairs(pair_rows)
    key_pos = lax.iota(jnp.int32, pair_rows.shape[0])
    clean_mask = visible_mask(clean_pos, key_pos, block_size, False)
    noisy_mask = visible_mask(noisy_pos, key_pos, block_size, True)

    def clean_update():
        return forward_step(carried[0], q_clean, key_rows, value_rows, clean_mask, score_scale)

    def clean_keep():
        return carried[0]

    def noisy_update():
        return forward_step(carried[1], q_noisy, key_rows, value_rows, noisy_mask, score_scale)

    def noisy_keep():
        return carried[1]

    clean_state = lax.cond(first_row < clean_limit, clean_update, clean_keep)
    noisy_state = lax.cond(first_row < noisy_limit, noisy_update, noisy_keep)
    clean_lse, clean_delta = finish_rows(clean_state, g_clean)
    noisy_lse, noisy_delta = finish_rows(noisy_state, g_noisy)
    pairs_back = lax.all_gather(clean_pairs, "context", axis=0, tiled=True)
    query_zero = jnp.zeros((shard_rows, kv_local, group_size, HEAD_DIM), jnp.float32)

    def backward_turn(turn_index, carried):
        query_grads, pair_total = carried
        first_row = turn_index * span_rows
        pair_rows = lax.dynamic_slice_in_dim(pairs_back, first_row, span_rows, 0)
        key_rows, value_rows = split_pairs(pair_rows)
        key_pos = first_row + lax.iota(jnp.int32, span_rows)
        clean_mask = visible_mask(clean_pos, key_pos, block_size, False)
        noisy_mask = visible_mask(noisy_pos, key_pos, block_size, True)
        pair_zero = jnp.zeros((span_rows, kv_local, HEAD_DIM), jnp.float32)

        def clean_work():
            return backward_step(
                q_clean,
                g_clean,
                key_rows,
                value_rows,
                clean_mask,
                clean_lse,
                clean_delta,
                score_scale,
            )

        def noisy_work():
            return backward_step(
                q_noisy,
                g_noisy,
                key_rows,
                value_rows,
                noisy_mask,
                noisy_lse,
                noisy_delta,
                score_scale,
            )

        def no_work():
            return (query_zero, pair_zero, pair_zero)

        clean_dq, clean_dk, clean_dv = lax.cond(first_row < clean_limit, clean_work, no_work)
        noisy_dq, noisy_dk, noisy_dv = lax.cond(first_row < noisy_limit, noisy_work, no_work)
        pair_grads = jnp.concatenate(
            [
                (clean_dk + noisy_dk).reshape(span_rows, kv_width),
                (clean_dv + noisy_dv).reshape(span_rows, kv_width),
            ],
            axis=1,
        )
        previous = lax.dynamic_slice_in_dim(pair_total, first_row, span_rows, 0)
        pair_total = lax.dynamic_update_slice_in_dim(
            pair_total, previous + pair_grads, first_row, 0
        )
        return ((query_grads[0] + clean_dq, query_grads[1] + noisy_dq), pair_total)

    pair_empty = jnp.zeros((cycle_size * shard_rows, 2 * kv_width), jnp.float32)
    query_grads, pair_total = lax.fori_loop(
        0, block_turns, backward_turn, ((query_zero, query_zero), pair_empty)
    )
    clean_pair_grads = lax.psum_scatter(
        pair_total.astype(jnp.bfloat16), "context", scatter_dimension=0, tiled=True
    )
    own_dq, own_dk, own_dv = backward_step(
        q_noisy, g_noisy, k_noisy, v_noisy, same_block, noisy_lse, noisy_delta, score_scale
    )
    dq_clean = (query_grads[0] * score_scale).astype(jnp.bfloat16).reshape(shard_rows, query_width)
    dq_noisy = (
        ((query_grads[1] + own_dq) * score_scale)
        .astype(jnp.bfloat16)
        .reshape(shard_rows, query_width)
    )
    noisy_pair = jnp.concatenate(
        [own_dk.reshape(shard_rows, kv_width), own_dv.reshape(shard_rows, kv_width)], axis=1
    ).astype(jnp.bfloat16)
    return_bundle = jnp.concatenate([dq_noisy, noisy_pair], axis=1)
    dq_noisy = return_bundle[:, :query_width]
    noisy_pair = return_bundle[:, query_width:]
    pair_grads = jnp.concatenate([clean_pair_grads, noisy_pair], axis=0)
    input_terms = jnp.einsum(
        "tc,rc->tr",
        pair_grads,
        lax.all_gather(weight_pair, "context", axis=0, tiled=True),
        preferred_element_type=jnp.float32,
    )
    grad_x = lax.psum_scatter(
        input_terms.astype(jnp.bfloat16), "head", scatter_dimension=1, tiled=True
    ).reshape(tokens.shape)
    columns = full_tokens
    weight_local = lax.psum_scatter(
        jnp.einsum("tr,tc->rc", columns, pair_grads, preferred_element_type=jnp.float32).astype(
            jnp.bfloat16
        ),
        "context",
        scatter_dimension=0,
        tiled=True,
    )
    weight_sums = lax.psum(weight_local, "dp").astype(jnp.float32)
    grad_query = jnp.stack([dq_clean, dq_noisy])[None]
    return (grad_query, grad_x, weight_sums[:, :kv_width], weight_sums[:, kv_width:])


def solution(mesh):
    placed = (
        P("dp", None, "context", "head"),
        P("dp", None, "context", "head"),
        P("dp", None, "context", "head"),
        P("context", "head"),
        P("context", "head"),
        P("dp"),
    )
    return jax.shard_map(
        per_device,
        mesh=mesh,
        in_specs=placed,
        out_specs=(
            P("dp", None, "context", "head"),
            P("dp", None, "context", "head"),
            P("context", "head"),
            P("context", "head"),
        ),
        check_vma=False,
    )
```

profile of v0, /device:TPU:0, one launch (start us, length us, event | category | flops | bytes accessed | tf_op | source)
XLA Modules:
  0.0 246.0 jit_solution(10116017296213389250)
XLA Ops:
  8.0 1.9 pad_maximum_fusion
  10.9 0.9 copy.91
  11.9 0.9 copy.89
  14.0 8.9 %all-gather.5.cloned.1.call-done = bf16[256,4096]{1,0:T(8,128)(2,1)} async-done(((bf16[256,2048]{1,0:T(8,128)(2,1)}), bf16[256,4096]{1,0:T(8,128)(2,1)}) %all-gather.5.cloned.1.call-update) | async-done | bytes 2097168 | tf_op jit(solution)/shard_map/all_gather | solution.py:84
  22.9 49.0 %all-gather.3.cloned.1.call-done = bf16[4096,256]{1,0:T(8,128)(2,1)} async-done(((bf16[1024,256]{1,0:T(8,128)(2,1)}), bf16[4096,256]{1,0:T(8,128)(2,1)}) %all-gather.3.cloned.1.call-update) | async-done | bytes 2097168 | tf_op jit(solution)/shard_map/all_gather | solution.py:91
  71.9 3.0 %fusion.88 = bf16[256,256]{0,1:T(8,128)(2,1)S(1)} fusion(bf16[4096,256]{1,0:T(8,128)(2,1)} %all-gather.3.cloned.1.call-done, bf16[256,4096]{1,0:T(8,128)(2,1)} %all-gather.5.cloned.1.call-done), kind=kOutput, calls=%fused_computation.128 | convolution fusion | flops 536936448 | bytes 4325376 | tf_op jit(solution)/shard_map/dot_general | solution.py:89
  74.9 13.4 %all_gather.13 = bf16[512,256]{0,1:T(8,128)(2,1)S(1)} all-gather(bf16[128,256]{0,1:T(8,128)(2,1)S(1)} %slice.67), channel_id=1, replica_groups=mesh['dp'=4,'context'=4,'head'=2] {'context'}, dimensions={0}, use_global_device_ids=true | all-gather | bytes 327680 | tf_op jit(solution)/shard_map/all_gather | solution.py:151
  91.2 2.9 %conditional.4 = (f32[1,8,128]{2,1,0:T(8,128)S(1)}, f32[1,8,128]{2,1,0:T(8,128)S(1)}, f32[1,8,128,128]{3,2,1,0:T(8,128)S(1)}, f32[1,8,128]{2,1,0:T(8,128)S(1)}) conditional(s32[]{:T(128)} %convert_element_type.73, () %tuple.57, (s32[512]{0:T(512)S(1)}, s32[128,512]{0,1:T(8,128)S(1)}, bf16[512,1,128]{0,2,1:T(8,128)(2,1)S(1)}, ...), branch_computations={%region_0.1_spmd, %region_1.4_spmd} | conditional | flops 275452928 | bytes 7919648 | solution.py:147
  92.4 1.7 fusion.7
  95.1 2.9 %conditional.5 = (f32[1,8,128]{2,1,0:T(8,128)S(1)}, f32[1,8,128]{2,1,0:T(8,128)S(1)}, f32[1,8,128,128]{3,2,1,0:T(8,128)S(1)}, f32[1,8,128]{2,1,0:T(8,128)S(1)}) conditional(s32[]{:T(128)} %convert_element_type.73, (f32[1,8,128]{2,1,0:T(8,128)S(1)}, f32[1,8,128]{2,1,0:T(8,128)S(1)}, f32[1,8,128,128]{3,2,1,0:T(8,128)S(1)}) %tuple.59, ...), branch_computations={%region_6.7_spmd, %region_7.10_spmd} | conditional | flops 275581952 | bytes 8460320 | solution.py:148
  95.8 1.7 fusion.26
  99.8 13.3 %while.20 = (s32[]{:T(128)}, f32[128,1,8,128]{3,0,2,1:T(8,128)}, f32[128,1,8,128]{3,0,2,1:T(8,128)S(1)}, f32[512,256]{1,0:T(8,128)S(1)}, s32[]{:T(128)}, /*index...) while((s32[]{:T(128)}, f32[128,1,8,128]{3,0,2,1:T(8,128)}, ...), condition=%wide.region_15.16_spmd.clone.clone, body=%wide.region_10.15_spmd.clone.clone.sunk | while | flops 1350440704 | bytes 32791988 | solution.py:207
  101.4 1.0 slice_bitcast_fusion.11
  102.4 4.5 %conditional.12 = (f32[128,1,8,128]{3,0,2,1:T(8,128)S(1)}, f32[512,1,128]{2,0,1:T(8,128)S(1)}, f32[512,1,128]{2,0,1:T(8,128)S(1)}) conditional(s32[]{:T(128)} %convert_element_type.129, () %tuple.125, (s32[512]{0:T(512)S(1)}, s32[128,512]{0,1:T(8,128)S(1)}, bf16[512,1,128]{2,0,1:T(8,128)(2,1)S(1)}, bf16[128,1,8,128]{3,0,2,1:T(8,128)(2,1)}, ...), branch_computations={%region_11.11_spmd, %region_12.12_spmd} | conditional | flops 674889728 | bytes 12331032 | solution.py:191
  102.6 1.5 fusion.45
  105.0 1.4 fusion.48
  106.9 1.9 add.307
  108.8 4.0 %conditional.13 = (f32[128,1,8,128]{3,0,2,1:T(8,128)S(1)}, f32[512,1,128]{2,0,1:T(8,128)S(1)}, f32[512,1,128]{2,0,1:T(8,128)S(1)}) conditional(s32[]{:T(128)} %convert_element_type.129, () %tuple.127, (s32[512]{0:T(512)S(1)}, s32[128,512]{0,1:T(8,128)S(1)}, bf16[512,1,128]{2,0,1:T(8,128)(2,1)S(1)}, bf16[128,1,8,128]{3,0,2,1:T(8,128)(2,1)}, ...), branch_computations={%region_13.13_spmd, %region_14.14_spmd} | conditional | flops 674889728 | bytes 13379636 | solution.py:192
  108.9 1.5 fusion.61
  114.2 1.4 fusion.87
  116.1 16.7 %reduce-scatter.10.cloned.1.call-done = bf16[128,256]{1,0:T(8,128)(2,1)} async-done(((bf16[512,256]{1,0:T(8,128)(2,1)}), bf16[128,256]{1,0:T(8,128)(2,1)}) %reduce-scatter.10.cloned.1.call-update) | async-done | bytes 65552
  132.8 0.9 copy.132
  133.7 3.7 %fusion.77 = bf16[4096,256]{0,1:T(8,128)(2,1)} fusion(bf16[256,4096]{1,0:T(8,128)(2,1)} %all-gather.5.cloned.1.call-done, bf16[128,128]{0,1:T(8,128)(2,1)S(1)} %fusion.90, bf16[128,128]{0,1:T(8,128)(2,1)S(1)} %fusion.91, bf16[128,256]{0,1:T(8,128)(2,1)S(1)} %copy.132), kind=kOutput, calls=%fused_computation.112 | convolution fusion | flops 538312704 | bytes 4325376 | tf_op jit(solution)/shard_map/tr,tc->rc/dot_general | solution.py:240
  137.5 41.9 %reduce-scatter.8.cloned.1.call-done = bf16[1024,256]{0,1:T(8,128)(2,1)} async-done(((bf16[4096,256]{0,1:T(8,128)(2,1)}), bf16[1024,256]{0,1:T(8,128)(2,1)}) %reduce-scatter.8.cloned.1.call-update) | async-done | bytes 524304 | tf_op jit(solution)/shard_map/reduce_scatter | solution.py:239
  179.5 2.1 convolution_convert_fusion.1
  181.6 1.0 copy-done
  183.3 1.0 fusion.84
  185.2 41.6 %all-reduce.2.cloned.1.call-done = bf16[1024,256]{0,1:T(8,128)(2,1)} async-done(((bf16[1024,256]{0,1:T(8,128)(2,1)}), bf16[1024,256]{0,1:T(8,128)(2,1)}) %all-reduce.2.cloned.1.call-update) | async-done | bytes 524304 | tf_op jit(solution)/shard_map/psum | solution.py:247
  226.9 1.1 fusion.111
  228.0 1.0 copy.104
  229.0 1.0 copy.103
  230.0 9.2 %reduce-scatter.6.cloned.1.call-done = bf16[256,2048]{1,0:T(8,128)(2,1)} async-done(((bf16[256,4096]{1,0:T(8,128)(2,1)}), bf16[256,2048]{1,0:T(8,128)(2,1)}) %reduce-scatter.6.cloned.1.call-update) | async-done | bytes 1048592 | tf_op jit(solution)/shard_map/reduce_scatter | solution.py:235
  (111 shorter events, 19.3 us)
Async XLA Ops:
  7.2 3.5 %copy-start.9 = (bf16[1,2,128,1024]{3,2,1,0:T(8,128)(2,1)S(1)}, bf16[1,2,128,1024]{3,2,1,0:T(8,128)(2,1)}, u32[]{:S(2)}) copy-start(bf16[1,2,128,1024]{3,2,1,0:T(8,128)(2,1)} %param.17) | copy-start | bytes 1572868
  7.2 15.7 %all-gather.5.cloned.1.call-start = ((), (), s32[]{:S(2)}) async-start(), calls=%async_computation.4 | async-start | bytes 3145728 | tf_op jit(solution)/shard_map/all_gather | solution.py:84
  7.9 64.0 %all-gather.3.cloned.1.call-start = ((), (), s32[]{:S(2)}) async-start(), calls=%async_computation.3 | async-start | bytes 2621440 | tf_op jit(solution)/shard_map/all_gather | solution.py:91
  9.8 2.9 %copy-start.10 = (bf16[1,2,128,1024]{3,2,1,0:T(8,128)(2,1)S(1)}, bf16[1,2,128,1024]{3,2,1,0:T(8,128)(2,1)}, u32[]{:S(2)}) copy-start(bf16[1,2,128,1024]{3,2,1,0:T(8,128)(2,1)} %param.18) | copy-start | bytes 1572868
  9.9 122.9 %reduce-scatter.10.cloned.1.call-start = ((), (), s32[]{:S(2)}) async-start(), calls=%async_computation.8 | async-start | bytes 327680
  10.8 84.3 %copy-start.4 = (bf16[1,1,128,1024]{2,3,1,0:T(8,128)(2,1)}, bf16[1,1,128,1024]{2,3,1,0:T(8,128)(2,1)S(1)}, u32[]{:S(2)}) copy-start(bf16[1,1,128,1024]{2,3,1,0:T(8,128)(2,1)S(1)} %copy.135) | copy-start | bytes 786436
  13.0 85.9 %copy-start.6 = (bf16[1,1,128,1024]{2,3,1,0:T(8,128)(2,1)}, bf16[1,1,128,1024]{2,3,1,0:T(8,128)(2,1)S(1)}, u32[]{:S(2)}) copy-start(bf16[1,1,128,1024]{2,3,1,0:T(8,128)(2,1)S(1)} %copy.136) | copy-start | bytes 786436
  74.8 16.4 %copy-start.11 = (bf16[256,256]{0,1:T(8,128)(2,1)}, bf16[256,256]{0,1:T(8,128)(2,1)S(1)}, u32[]{:S(2)}) copy-start(bf16[256,256]{0,1:T(8,128)(2,1)S(1)} %fusion.88) | copy-start | bytes 393220
  90.1 0.8 copy-start.1
  94.1 0.6 copy-start.12
  94.1 0.6 copy-start.14
  98.0 0.7 copy-start.13
  98.1 0.7 copy-start.15
  110.9 1.0 copy-start.3
  113.1 2.5 %copy-start.5 = (bf16[1,1,128,1024]{2,3,1,0:T(8,128)(2,1)S(1)}, bf16[1,1,128,1024]{2,3,1,0:T(8,128)(2,1)}, u32[]{:S(2)}) copy-start(bf16[1,1,128,1024]{2,3,1,0:T(8,128)(2,1)} %copy-done.4) | copy-start | bytes 786436
  113.1 2.7 %copy-start.2 = (f32[1,8,128,128]{2,3,1,0:T(8,128)S(1)}, f32[1,8,128,128]{2,3,1,0:T(8,128)}, u32[]{:S(2)}) copy-start(f32[1,8,128,128]{2,3,1,0:T(8,128)} %copy-done.1) | copy-start | bytes 1572868
  113.1 2.7 %copy-start.7 = (bf16[1,1,128,1024]{2,3,1,0:T(8,128)(2,1)S(1)}, bf16[1,1,128,1024]{2,3,1,0:T(8,128)(2,1)}, u32[]{:S(2)}) copy-start(bf16[1,1,128,1024]{2,3,1,0:T(8,128)(2,1)} %copy-done.6) | copy-start | bytes 786436
  114.1 65.3 %reduce-scatter.8.cloned.1.call-start = ((), (), s32[]{:S(2)}) async-start(), calls=%async_computation.6 | async-start | bytes 2621440 | tf_op jit(solution)/shard_map/reduce_scatter | solution.py:239
  137.4 42.1 %copy-start.8 = (bf16[4096,256]{1,0:T(8,128)(2,1)S(1)}, bf16[4096,256]{1,0:T(8,128)(2,1)}, u32[]{:S(2)}) copy-start(bf16[4096,256]{1,0:T(8,128)(2,1)} %all-gather.3.cloned.1.call-done) | copy-start | bytes 6291460
  137.4 89.4 %all-reduce.2.cloned.1.call-start = ((), (), s32[]{:S(2)}) async-start(), calls=%async_computation.7 | async-start | bytes 1048576 | tf_op jit(solution)/shard_map/psum | solution.py:247
  179.4 59.7 %reduce-scatter.6.cloned.1.call-start = ((), (), s32[]{:S(2)}) async-start(), calls=%async_computation.5 | async-start | bytes 3145728 | tf_op jit(solution)/shard_map/reduce_scatter | solution.py:235
  181.6 1.0 copy-start
Sparse Core Ops, SparseCore 0:
  9.5 13.2 all-gather.4
  25.0 46.8 all-gather.2
  114.3 18.4 reduce-scatter.9
  137.5 41.8 reduce-scatter.7
  182.3 44.5 all-reduce.1
  229.5 9.6 reduce-scatter.5
where the time goes:
time: 247 us; the launch traced here: 246 us
  waiting for transfers between devices  168 us (68%)
  matrix products  24.1 us (10%)
  local copies, waits for them, and re-layouts  15.5 us (6%)
  between operations  15.3 us (6%)
  blocking collectives  13.4 us (5%)
  other arithmetic  9.27 us (4%)
    all_gather x1, waiting for transfers between devices, per_device(): lax.all_gather(weight_pair, 'context', axis=0, tiled=True)  49 us
    reduce_scatter x1, waiting for transfers between devices, per_device(): lax.psum_scatter(jnp.einsum('tr,tc->rc', columns, pair_grads, preferred_e...  41.9 us
    psum x1, waiting for transfers between devices, per_device(): weight_sums = lax.psum(weight_local, 'dp').astype(jnp.float32)  41.6 us
    unnamed x7, waiting for transfers between devices  17.4 us
    all_gather x1, blocking collectives, per_device(): pairs_back = lax.all_gather(clean_pairs, 'context', axis=0, tiled=True)  13.4 us
    unnamed x45, local copies, waits for them, and re-layouts  10.3 us
    reduce_scatter x1, waiting for transfers between devices, per_device(): lax.psum_scatter(input_terms.astype(jnp.bfloat16), 'head', scatter_dimens...  9.19 us
    all_gather x1, waiting for transfers between devices, per_device(): lax.all_gather(tokens[0].reshape(2 * shard_rows, tokens.shape[3]), 'head'...  8.85 us
  transfers between devices with their start and end apart: 6, of which 6 were waited for; matrix products, arithmetic and copies ran while one was open for 6% of the time, Pallas kernels for 0%

commit v1 on v0

--- a/solution.py
+++ b/solution.py
@@ -244,7 +244,7 @@
         scatter_dimension=0,
         tiled=True,
     )
-    weight_sums = lax.psum(weight_local, "dp").astype(jnp.float32)
+    weight_sums = jnp.sum(lax.all_gather(weight_local, "dp"), axis=0).astype(jnp.float32)
     grad_query = jnp.stack([dq_clean, dq_noisy])[None]
     return (grad_query, grad_x, weight_sums[:, :kv_width], weight_sums[:, kv_width:])
 

time: 247 us -> 235 us (0.951)
  waiting for transfers between devices: 168 us -> 152 us
  other arithmetic: 9.27 us -> 12.1 us
    psum x1 -> x0, waiting for transfers between devices: 41.6 us -> none  [per_device(): weight_sums = lax.psum(weight_local, 'dp').astype(jnp.float32)]
    all_gather x0 -> x1, waiting for transfers between devices: none -> 30.3 us  [per_device(): lax.all_gather(weight_local, 'dp')]
    reduce_scatter x1, waiting for transfers between devices: 9.19 us -> 4.04 us  [per_device(): lax.psum_scatter(input_terms.astype(jnp.bfloat16), 'head', scatter_dimens...]
    all_gather x0 -> x1, local copies, waits for them, and re-layouts: none -> 3.32 us  [per_device(): lax.all_gather(weight_local, 'dp')]
    reduce_sum x0 -> x1, other arithmetic: none -> 2.85 us  [per_device(): jnp.sum(lax.all_gather(weight_local, 'dp'), axis=0).astype(jnp.float32)]
  transfers between devices with their start and end apart: 6 -> 6, of which waited for: 6 -> 6; matrix products, arithmetic and copies ran while one was open for 6% -> 9% of each run, Pallas kernels for 0% -> 0%
where the time goes in v1:
time: 235 us
  waiting for transfers between devices  152 us (65%)
  matrix products  24.1 us (10%)
  local copies, waits for them, and re-layouts  17.8 us (8%)
  between operations  15.2 us (6%)
  blocking collectives  13.4 us (6%)
  other arithmetic  12.1 us (5%)
    all_gather x1, waiting for transfers between devices, per_device(): lax.all_gather(weight_pair, 'context', axis=0, tiled=True)  49 us
    reduce_scatter x1, waiting for transfers between devices, per_device(): lax.psum_scatter(jnp.einsum('tr,tc->rc', columns, pair_grads, preferred_e...  41.9 us
    all_gather x1, waiting for transfers between devices, per_device(): lax.all_gather(weight_local, 'dp')  30.3 us
    unnamed x7, waiting for transfers between devices  17.4 us
    all_gather x1, blocking collectives, per_device(): pairs_back = lax.all_gather(clean_pairs, 'context', axis=0, tiled=True)  13.4 us
    unnamed x45, local copies, waits for them, and re-layouts  10.3 us
    all_gather x1, waiting for transfers between devices, per_device(): lax.all_gather(tokens[0].reshape(2 * shard_rows, tokens.shape[3]), 'head'...  8.87 us
  transfers between devices with their start and end apart: 6, of which 6 were waited for; matrix products, arithmetic and copies ran while one was open for 9% of the time, Pallas kernels for 0%

profile of v1, /device:TPU:0, one launch (start us, length us, event | category | flops | bytes accessed | tf_op | source)
XLA Modules:
  0.0 234.7 jit_solution(7636238975362787115)
XLA Ops:
  8.0 1.9 pad_maximum_fusion
  11.9 0.9 copy.85
  14.0 8.9 %all-gather.7.cloned.1.call-done = bf16[256,4096]{1,0:T(8,128)(2,1)} async-done(((bf16[256,2048]{1,0:T(8,128)(2,1)}), bf16[256,4096]{1,0:T(8,128)(2,1)}) %all-gather.7.cloned.1.call-update) | async-done | bytes 2097168 | tf_op jit(solution)/shard_map/all_gather | solution.py:84
  22.9 49.0 %all-gather.5.cloned.1.call-done = bf16[4096,256]{1,0:T(8,128)(2,1)} async-done(((bf16[1024,256]{1,0:T(8,128)(2,1)}), bf16[4096,256]{1,0:T(8,128)(2,1)}) %all-gather.5.cloned.1.call-update) | async-done | bytes 2097168 | tf_op jit(solution)/shard_map/all_gather | solution.py:91
  71.9 3.0 %fusion.88 = bf16[256,256]{0,1:T(8,128)(2,1)S(1)} fusion(bf16[4096,256]{1,0:T(8,128)(2,1)} %all-gather.5.cloned.1.call-done, bf16[256,4096]{1,0:T(8,128)(2,1)} %all-gather.7.cloned.1.call-done), kind=kOutput, calls=%fused_computation.128 | convolution fusion | flops 536936448 | bytes 4325376 | tf_op jit(solution)/shard_map/dot_general | solution.py:89
  74.9 13.4 %all_gather.19 = bf16[512,256]{0,1:T(8,128)(2,1)S(1)} all-gather(bf16[128,256]{0,1:T(8,128)(2,1)S(1)} %slice.67), channel_id=1, replica_groups=mesh['dp'=4,'context'=4,'head'=2] {'context'}, dimensions={0}, use_global_device_ids=true | all-gather | bytes 327680 | tf_op jit(solution)/shard_map/all_gather | solution.py:151
  91.2 2.9 %conditional.4 = (f32[1,8,128]{2,1,0:T(8,128)S(1)}, f32[1,8,128]{2,1,0:T(8,128)S(1)}, f32[1,8,128,128]{3,2,1,0:T(8,128)S(1)}, f32[1,8,128]{2,1,0:T(8,128)S(1)}) conditional(s32[]{:T(128)} %convert_element_type.75, () %tuple.57, (s32[512]{0:T(512)S(1)}, s32[128,512]{0,1:T(8,128)S(1)}, bf16[512,1,128]{0,2,1:T(8,128)(2,1)S(1)}, ...), branch_computations={%region_0.1_spmd, %region_1.4_spmd} | conditional | flops 275452928 | bytes 7919648 | solution.py:147
  92.4 1.7 fusion.7
  95.1 2.9 %conditional.5 = (f32[1,8,128]{2,1,0:T(8,128)S(1)}, f32[1,8,128]{2,1,0:T(8,128)S(1)}, f32[1,8,128,128]{3,2,1,0:T(8,128)S(1)}, f32[1,8,128]{2,1,0:T(8,128)S(1)}) conditional(s32[]{:T(128)} %convert_element_type.75, (f32[1,8,128]{2,1,0:T(8,128)S(1)}, f32[1,8,128]{2,1,0:T(8,128)S(1)}, f32[1,8,128,128]{3,2,1,0:T(8,128)S(1)}) %tuple.59, ...), branch_computations={%region_6.7_spmd, %region_7.10_spmd} | conditional | flops 275581952 | bytes 8460320 | solution.py:148
  95.8 1.7 fusion.26
  99.8 13.3 %while.20 = (s32[]{:T(128)}, f32[128,1,8,128]{3,0,2,1:T(8,128)}, f32[128,1,8,128]{3,0,2,1:T(8,128)S(1)}, f32[512,256]{1,0:T(8,128)S(1)}, s32[]{:T(128)}, /*index...) while((s32[]{:T(128)}, f32[128,1,8,128]{3,0,2,1:T(8,128)}, ...), condition=%wide.region_15.16_spmd.clone.clone, body=%wide.region_10.15_spmd.clone.clone.sunk | while | flops 1350440704 | bytes 32791988 | solution.py:207
  101.4 1.0 slice_bitcast_fusion.11
  102.4 4.5 %conditional.12 = (f32[128,1,8,128]{3,0,2,1:T(8,128)S(1)}, f32[512,1,128]{2,0,1:T(8,128)S(1)}, f32[512,1,128]{2,0,1:T(8,128)S(1)}) conditional(s32[]{:T(128)} %convert_element_type.131, () %tuple.123, (s32[512]{0:T(512)S(1)}, s32[128,512]{0,1:T(8,128)S(1)}, bf16[512,1,128]{2,0,1:T(8,128)(2,1)S(1)}, bf16[128,1,8,128]{3,0,2,1:T(8,128)(2,1)}, ...), branch_computations={%region_11.11_spmd, %region_12.12_spmd} | conditional | flops 674889728 | bytes 12331032 | solution.py:191
  102.6 1.5 fusion.45
  105.0 1.4 fusion.48
  106.9 1.9 add.305
  108.8 4.0 %conditional.13 = (f32[128,1,8,128]{3,0,2,1:T(8,128)S(1)}, f32[512,1,128]{2,0,1:T(8,128)S(1)}, f32[512,1,128]{2,0,1:T(8,128)S(1)}) conditional(s32[]{:T(128)} %convert_element_type.131, () %tuple.125, (s32[512]{0:T(512)S(1)}, s32[128,512]{0,1:T(8,128)S(1)}, bf16[512,1,128]{2,0,1:T(8,128)(2,1)S(1)}, bf16[128,1,8,128]{3,0,2,1:T(8,128)(2,1)}, ...), branch_computations={%region_13.13_spmd, %region_14.14_spmd} | conditional | flops 674889728 | bytes 13379636 | solution.py:192
  108.9 1.5 fusion.61
  114.2 1.4 fusion.87
  116.1 16.7 %reduce-scatter.10.cloned.1.call-done = bf16[128,256]{1,0:T(8,128)(2,1)} async-done(((bf16[512,256]{1,0:T(8,128)(2,1)}), bf16[128,256]{1,0:T(8,128)(2,1)}) %reduce-scatter.10.cloned.1.call-update) | async-done | bytes 65552
  132.8 0.9 copy.128
  133.7 3.7 %fusion.77 = bf16[4096,256]{0,1:T(8,128)(2,1)} fusion(bf16[256,4096]{1,0:T(8,128)(2,1)} %all-gather.7.cloned.1.call-done, bf16[128,128]{0,1:T(8,128)(2,1)S(1)} %fusion.90, bf16[128,128]{0,1:T(8,128)(2,1)S(1)} %fusion.91, bf16[128,256]{0,1:T(8,128)(2,1)S(1)} %copy.128), kind=kOutput, calls=%fused_computation.112 | convolution fusion | flops 538312704 | bytes 4325376 | tf_op jit(solution)/shard_map/tr,tc->rc/dot_general | solution.py:240
  137.5 41.9 %reduce-scatter.8.cloned.1.call-done = bf16[1024,256]{0,1:T(8,128)(2,1)} async-done(((bf16[4096,256]{0,1:T(8,128)(2,1)}), bf16[1024,256]{0,1:T(8,128)(2,1)}) %reduce-scatter.8.cloned.1.call-update) | async-done | bytes 524304 | tf_op jit(solution)/shard_map/reduce_scatter | solution.py:239
  179.5 2.1 convolution_convert_fusion.1
  181.6 1.0 copy-done
  183.3 1.0 fusion.84
  185.3 30.3 %all-gather.9.cloned.1.call-done = bf16[4096,256]{0,1:T(8,128)(2,1)} async-done(((bf16[1024,256]{0,1:T(8,128)(2,1)}), bf16[4096,256]{0,1:T(8,128)(2,1)}) %all-gather.9.cloned.1.call-update) | async-done | bytes 2097168 | tf_op jit(solution)/shard_map/all_gather | solution.py:247
  215.5 3.3 %reshape.438 = bf16[4,1024,256]{1,0,2:T(4,128)(2,1)S(1)} reshape(bf16[4096,256]{0,1:T(8,128)(2,1)} %all-gather.9.cloned.1.call-done) | data formatting | bytes 4194304 | tf_op jit(solution)/shard_map/all_gather | solution.py:247
  218.9 2.8 %reduce_sum.47 = bf16[1024,256]{0,1:T(8,128)(2,1)S(1)} reduce(bf16[4,1024,256]{1,0,2:T(4,128)(2,1)S(1)} %reshape.438, bf16[]{:T(256)} %constant.139.clone.1), dimensions={0}, to_apply=%region_19.20 | reduce | flops 786432 | bytes 2621442 | tf_op jit(solution)/shard_map/reduce_sum | solution.py:247
  221.8 1.0 copy.100
  222.8 1.0 copy.99
  223.8 4.0 %reduce-scatter.6.cloned.1.call-done = bf16[256,2048]{1,0:T(8,128)(2,1)} async-done(((bf16[256,4096]{1,0:T(8,128)(2,1)}), bf16[256,2048]{1,0:T(8,128)(2,1)}) %reduce-scatter.6.cloned.1.call-update) | async-done | bytes 1048592 | tf_op jit(solution)/shard_map/reduce_scatter | solution.py:235
  (113 shorter events, 20.3 us)
Async XLA Ops:
  7.2 3.5 %copy-start.9 = (bf16[1,2,128,1024]{3,2,1,0:T(8,128)(2,1)S(1)}, bf16[1,2,128,1024]{3,2,1,0:T(8,128)(2,1)}, u32[]{:S(2)}) copy-start(bf16[1,2,128,1024]{3,2,1,0:T(8,128)(2,1)} %param.17) | copy-start | bytes 1572868
  7.2 15.7 %all-gather.7.cloned.1.call-start = ((), (), s32[]{:S(2)}) async-start(), calls=%async_computation.4 | async-start | bytes 3145728 | tf_op jit(solution)/shard_map/all_gather | solution.py:84
  7.9 64.0 %all-gather.5.cloned.1.call-start = ((), (), s32[]{:S(2)}) async-start(), calls=%async_computation.3 | async-start | bytes 2621440 | tf_op jit(solution)/shard_map/all_gather | solution.py:91
  9.8 2.9 %copy-start.10 = (bf16[1,2,128,1024]{3,2,1,0:T(8,128)(2,1)S(1)}, bf16[1,2,128,1024]{3,2,1,0:T(8,128)(2,1)}, u32[]{:S(2)}) copy-start(bf16[1,2,128,1024]{3,2,1,0:T(8,128)(2,1)} %param.18) | copy-start | bytes 1572868
  9.9 122.9 %reduce-scatter.10.cloned.1.call-start = ((), (), s32[]{:S(2)}) async-start(), calls=%async_computation.8 | async-start | bytes 327680
  10.8 84.3 %copy-start.4 = (bf16[1,1,128,1024]{2,3,1,0:T(8,128)(2,1)}, bf16[1,1,128,1024]{2,3,1,0:T(8,128)(2,1)S(1)}, u32[]{:S(2)}) copy-start(bf16[1,1,128,1024]{2,3,1,0:T(8,128)(2,1)S(1)} %copy.131) | copy-start | bytes 786436
  13.0 85.9 %copy-start.6 = (bf16[1,1,128,1024]{2,3,1,0:T(8,128)(2,1)}, bf16[1,1,128,1024]{2,3,1,0:T(8,128)(2,1)S(1)}, u32[]{:S(2)}) copy-start(bf16[1,1,128,1024]{2,3,1,0:T(8,128)(2,1)S(1)} %copy.132) | copy-start | bytes 786436
  74.8 16.4 %copy-start.11 = (bf16[256,256]{0,1:T(8,128)(2,1)}, bf16[256,256]{0,1:T(8,128)(2,1)S(1)}, u32[]{:S(2)}) copy-start(bf16[256,256]{0,1:T(8,128)(2,1)S(1)} %fusion.88) | copy-start | bytes 393220
  90.1 0.8 copy-start.1
  94.1 0.6 copy-start.12
  94.1 0.6 copy-start.14
  98.1 0.7 copy-start.13
  98.1 0.7 copy-start.15
  110.9 1.0 copy-start.3
  113.1 2.5 %copy-start.5 = (bf16[1,1,128,1024]{2,3,1,0:T(8,128)(2,1)S(1)}, bf16[1,1,128,1024]{2,3,1,0:T(8,128)(2,1)}, u32[]{:S(2)}) copy-start(bf16[1,1,128,1024]{2,3,1,0:T(8,128)(2,1)} %copy-done.4) | copy-start | bytes 786436
  113.1 2.7 %copy-start.2 = (f32[1,8,128,128]{2,3,1,0:T(8,128)S(1)}, f32[1,8,128,128]{2,3,1,0:T(8,128)}, u32[]{:S(2)}) copy-start(f32[1,8,128,128]{2,3,1,0:T(8,128)} %copy-done.1) | copy-start | bytes 1572868
  113.1 2.7 %copy-start.7 = (bf16[1,1,128,1024]{2,3,1,0:T(8,128)(2,1)S(1)}, bf16[1,1,128,1024]{2,3,1,0:T(8,128)(2,1)}, u32[]{:S(2)}) copy-start(bf16[1,1,128,1024]{2,3,1,0:T(8,128)(2,1)} %copy-done.6) | copy-start | bytes 786436
  114.1 65.3 %reduce-scatter.8.cloned.1.call-start = ((), (), s32[]{:S(2)}) async-start(), calls=%async_computation.6 | async-start | bytes 2621440 | tf_op jit(solution)/shard_map/reduce_scatter | solution.py:239
  137.4 42.1 %copy-start.8 = (bf16[4096,256]{1,0:T(8,128)(2,1)S(1)}, bf16[4096,256]{1,0:T(8,128)(2,1)}, u32[]{:S(2)}) copy-start(bf16[4096,256]{1,0:T(8,128)(2,1)} %all-gather.5.cloned.1.call-done) | copy-start | bytes 6291460
  137.4 78.1 %all-gather.9.cloned.1.call-start = ((), (), s32[]{:S(2)}) async-start(), calls=%async_computation.7 | async-start | bytes 2621440 | tf_op jit(solution)/shard_map/all_gather | solution.py:247
  179.5 48.4 %reduce-scatter.6.cloned.1.call-start = ((), (), s32[]{:S(2)}) async-start(), calls=%async_computation.5 | async-start | bytes 3145728 | tf_op jit(solution)/shard_map/reduce_scatter | solution.py:235
  181.6 1.0 copy-start
Sparse Core Ops, SparseCore 0:
  9.5 13.2 all-gather.6
  25.0 46.8 all-gather.4
  114.3 18.4 reduce-scatter.9
  137.6 41.8 reduce-scatter.7
  181.1 34.3 all-gather.8
  218.2 9.6 reduce-scatter.5
